TPU v7x, 32 devices: a whole 2x2x4 slice. The times are simulated.
32 devices in a mesh: gx: 4 (over x, core), gy: 8 (over z, y).
Axes of the slice: x: 2, y: 2, z: 4, core: 2. Of those that a mesh axis runs over, the one named last changes fastest.
Arguments:
- hot_ids: int32 [262144], P(('gx', 'gy')), may hold values from 0 to 2047
- hot_grads: bfloat16 [262144, 128], P(('gx', 'gy')), may hold values from -6 to 6
- cold_grads: bfloat16 [4, 8, 8, 512, 128], P('gx', 'gy'), may hold values from -6 to 6
- cold_slots: int32 [4, 8, 8, 512], P('gx', 'gy'), may hold values from 0 to 2047
- cold_counts: int32 [4, 8, 8], P('gx', 'gy'), may hold values from 1 to 512, as said below
Outputs:
- hot_grad: float32 [2048, 128], replicated
- cold_grad: float32 [4, 16384, 128], P('gx', 'gy')
Inputs may be any that keep to these rules, and one draw needn't show every extreme that they name: In each group g, some owner d receives cold_counts[g, s, d] = 512 from every s; loads per owner are skewed.
All inputs are finite; a program needn't handle non-finite values.
Results may differ from a plain program's by a relative error of at most 0.0003.
Values may be sent and summed in bfloat16 or wider, within the bound.
A program may use at most 64 MiB of HBM per device.

v0:
```python
import functools

import jax
import jax.numpy as jnp
from jax import lax
from jax.experimental import pallas as pl
from jax.experimental.pallas import tpu as pltpu
from jax.sharding import PartitionSpec as P

HOT = 2048
OWN_ROWS = 2048
LANES = 128
HIGH = 4
MESH = pl.DeviceIdType.MESH


def add_block(acc, ids, data, pieces, low_rows):
    columns = ids.T
    lo_iota = lax.broadcasted_iota(jnp.int32, (low_rows, LANES), 0)
    selectors, rows = [], []
    for j in range(pieces):
        lo = jnp.bitwise_and(ids[j : j + 1, :], low_rows - 1)
        selectors.append(jnp.where(lo_iota == lo, 1.0, 0.0).astype(jnp.bfloat16))
        here = data[j * LANES : (j + 1) * LANES, :]
        column = jnp.broadcast_to(columns[:, j : j + 1], here.shape)
        parts = []
        for h in range(HIGH):
            inside = (column >= h * low_rows) & (column < (h + 1) * low_rows)
            parts.append(here * jnp.where(inside, 1.0, 0.0).astype(jnp.bfloat16))
        rows.append(jnp.concatenate(parts, axis=1))
    selector = jnp.concatenate(selectors, axis=1)
    spread = jnp.concatenate(rows, axis=0)
    acc[...] += jnp.dot(selector, spread, preferred_element_type=jnp.float32)


def kernel(
    nx, ny, factor, cap_pieces,
    ids_ref, hot_ref, slots_ref, cold_ref, hot_out, cold_out,
    acc, cacc, tab, full, hotv, idsv, crecv, srecv, r0, a1, b1, a2, b2, a3, b3,
    csend, crsem, ssend, srsem, own_sem, hsend, hrecv,
):
    gx, gy = lax.axis_index("gx"), lax.axis_index("gy")
    px, py = 2 - nx % 2, 2 - ny % 2
    low_rows = HOT // HIGH
    own_low = OWN_ROWS // HIGH
    width = hot_ref.shape[1]
    landing_refs = (a1, b1, a2, b2, a3, b3)

    core = (px, lax.rem(gx, px), lambda p: ((gx // px) * px + p, gy))
    along_x = (nx // px, gx // px, lambda p: (p * px + lax.rem(gx, px), gy))
    pair_y = (py, lax.rem(gy, py), lambda p: (gx, (gy // py) * py + p))
    rest_y = (ny // py, gy // py, lambda p: (gx, p * py + lax.rem(gy, py)))
    chains = [[along_x, pair_y, rest_y], [pair_y, along_x, rest_y]]

    hot_copy = pltpu.make_async_copy(hot_ref, hotv, own_sem.at[1])
    ids_copy = pltpu.make_async_copy(ids_ref, idsv, own_sem.at[2])
    own = pltpu.make_async_copy(cold_ref.at[gy], crecv.at[0], own_sem.at[0])
    ids_copy.start()
    hot_copy.start()

    barrier = pltpu.get_barrier_semaphore()
    greeted = 0
    for n, k, device in (core, along_x):
        for j in range(1, n):
            pl.semaphore_signal(barrier, inc=1, device_id=device(lax.rem(k + j, n)), device_id_type=MESH)
            greeted += 1
    for j in range(1, ny):
        pl.semaphore_signal(barrier, inc=1, device_id=(gx, lax.rem(gy + j, ny)), device_id_type=MESH)
        greeted += 1
    pl.semaphore_wait(barrier, greeted)

    def cold_copies(j):
        peer = lax.rem(gy + j, ny)
        return (
            pltpu.make_async_remote_copy(
                src_ref=cold_ref.at[peer], dst_ref=crecv.at[j],
                send_sem=csend.at[j], recv_sem=crsem.at[j],
                device_id=(gx, peer), device_id_type=MESH,
            ),
            pltpu.make_async_remote_copy(
                src_ref=slots_ref.at[peer], dst_ref=srecv.at[j],
                send_sem=ssend.at[j], recv_sem=srsem.at[j],
                device_id=(gx, peer), device_id_type=MESH,
            ),
        )

    middle = ny // 2
    for j in range(1, ny):
        if j != middle:
            for copy in cold_copies(j):
                copy.start()
    own.start()

    acc[...] = jnp.zeros_like(acc)
    cacc[...] = jnp.zeros_like(cacc)
    ids_copy.wait()
    hot_copy.wait()

    def hot_step(i, carry):
        pieces = idsv.shape[1]
        data = hotv[pl.ds(pl.multiple_of(i * pieces * LANES, LANES), pieces * LANES), :]
        add_block(acc, idsv[i], data, pieces, low_rows)
        return carry

    lax.fori_loop(0, idsv.shape[0], hot_step, 0)
    for h in range(HIGH):
        tab[h * low_rows : (h + 1) * low_rows, :] = acc[:, h * width : (h + 1) * width]

    used = 0

    def scatter_start(stage, base, size, landing):
        nonlocal used
        n, k, device = stage
        sub = size // n
        copies = []
        for j in range(1, n):
            peer = lax.rem(k + j, n)
            copies.append(
                pltpu.make_async_remote_copy(
                    src_ref=tab.at[pl.ds(pl.multiple_of(base + peer * sub, 8), sub), :],
                    dst_ref=landing.at[j - 1],
                    send_sem=hsend.at[used], recv_sem=hrecv.at[used],
                    device_id=device(peer), device_id_type=MESH,
                )
            )
            copies[-1].start()
            used += 1
        return copies

    def scatter_end(copies, stage, base, size, landing):
        n, k, device = stage
        for copy in copies:
            copy.wait()
        sub = size // n
        base = base + k * sub
        if n > 1:
            rows = pl.ds(pl.multiple_of(base, 8), sub)
            total = tab[rows, :]
            for j in range(1, n):
                total = total + landing[j - 1]
            tab[rows, :] = total
        return base, sub

    def gather_start(stage, base, size):
        nonlocal used
        n, k, device = stage
        rows = pl.ds(pl.multiple_of(base, 8), size)
        first = used
        for j in range(1, n):
            pltpu.make_async_remote_copy(
                src_ref=full.at[rows, :], dst_ref=full.at[rows, :],
                send_sem=hsend.at[used], recv_sem=hrecv.at[used],
                device_id=device(lax.rem(k + j, n)), device_id_type=MESH,
            ).start()
            used += 1
        return first

    def gather_end(first, stage, base, size):
        n, k, device = stage
        for j in range(1, n):
            mine = pl.ds(pl.multiple_of(base, 8), size)
            theirs = pl.ds(pl.multiple_of(base + (lax.rem(k - j + n, n) - k) * size, 8), size)
            for rows, receive in ((mine, False), (theirs, True)):
                copy = pltpu.make_async_remote_copy(
                    src_ref=full.at[rows, :], dst_ref=full.at[rows, :],
                    send_sem=hsend.at[first + j - 1], recv_sem=hrecv.at[first + j - 1],
                    device_id=device(lax.rem(k + j, n)), device_id_type=MESH,
                )
                if receive:
                    copy.wait_recv()
                else:
                    copy.wait_send()

    def cold_range(start, stop):
        def cold_step(j, carry):
            for copy in cold_copies(j):
                copy.wait()
            add_block(cacc, srecv[j], crecv[j], cap_pieces, own_low)
            return carry

        lax.fori_loop(start, stop, cold_step, 0)

    copies = scatter_start(core, 0, HOT, r0)
    own.wait()
    add_block(cacc, slots_ref[gy], crecv[0], cap_pieces, own_low)
    base, size = scatter_end(copies, core, 0, HOT, r0)
    top = (base, size)
    half = size // 2
    places = [(base, half), (base + half, half)]
    history = []
    for step in range(3):
        landings = [landing_refs[2 * step], landing_refs[2 * step + 1]]
        history.append(list(places))
        pending = [
            scatter_start(chains[c][step], *places[c], landings[c]) for c in range(2)
        ]
        places = [
            scatter_end(pending[c], chains[c][step], *places[c], landings[c]) for c in range(2)
        ]
    for place, size in places:
        rows = pl.ds(pl.multiple_of(place, 8), size)
        full[rows, :] = tab[rows, :] * factor
    for step in (2, 1, 0):
        firsts = [gather_start(chains[c][step], *places[c]) for c in range(2)]
        if step == 1:
            for copy in cold_copies(middle):
                copy.start()
            cold_range(1, middle)
        if step == 0:
            cold_range(middle + 1, ny)
        for c in range(2):
            gather_end(firsts[c], chains[c][step], *places[c])
        places = history[step]
    first = gather_start(core, *top)
    cold_range(middle, middle + 1)
    for h in range(HIGH):
        cold_out[h * own_low : (h + 1) * own_low, :] = cacc[:, h * width : (h + 1) * width]
    gather_end(first, core, *top)
    hot_out[...] = full[...]


def per_device(nx, ny, hot_ids, hot_grads, cold_grads, cold_slots, cold_counts):
    look, width = hot_grads.shape
    owners, capacity = cold_slots.shape[2], cold_slots.shape[3]
    px, py = 2 - nx % 2, 2 - ny % 2
    factor = (HOT / (look * nx * ny)) ** 0.5
    places = lax.broadcasted_iota(jnp.int32, (owners, capacity), 1)
    slots = jnp.where(places < cold_counts.reshape(owners, 1), cold_slots.reshape(owners, capacity), -1)
    cap_pieces = capacity // LANES
    slots = slots.reshape(owners, cap_pieces, LANES)
    pad = -cap_pieces % 8
    slots = jnp.pad(slots, ((0, 0), (0, pad), (0, 0)), constant_values=-1)
    ids = hot_ids.reshape(-1, 8, LANES)
    nxr, nyr = nx // px, ny // py
    s0 = HOT // px
    half = s0 // 2
    n_hot = 2 * ((px - 1) + 2 * ((nxr - 1) + (py - 1) + (nyr - 1)))

    def landing(n, rows):
        return pltpu.VMEM((max(n - 1, 1), rows // n, width), f32)

    f32 = jnp.float32
    hbm = pl.BlockSpec(memory_space=pltpu.HBM)
    vmem = pl.BlockSpec(memory_space=pltpu.VMEM)
    hot, cold = pl.pallas_call(
        functools.partial(kernel, nx, ny, factor, cap_pieces),
        out_shape=(
            jax.ShapeDtypeStruct((HOT, width), f32),
            jax.ShapeDtypeStruct((OWN_ROWS, width), f32),
        ),
        in_specs=[hbm, hbm, vmem, hbm],
        out_specs=(vmem, vmem),
        scratch_shapes=[
            pltpu.VMEM((HOT // HIGH, HIGH * width), f32),
            pltpu.VMEM((OWN_ROWS // HIGH, HIGH * width), f32),
            pltpu.VMEM((HOT, width), f32),
            pltpu.VMEM((HOT, width), f32),
            pltpu.VMEM((look, width), jnp.bfloat16),
            pltpu.VMEM(ids.shape, jnp.int32),
            pltpu.VMEM((owners, capacity, width), jnp.bfloat16),
            pltpu.VMEM((owners, cap_pieces + pad, LANES), jnp.int32),
            landing(px, HOT),
            landing(nxr, half),
            landing(py, half),
            landing(py, half // nxr),
            landing(nxr, half // py),
            landing(nyr, half // nxr // py),
            landing(nyr, half // nxr // py),
            pltpu.SemaphoreType.DMA((owners,)),
            pltpu.SemaphoreType.DMA((owners,)),
            pltpu.SemaphoreType.DMA((owners,)),
            pltpu.SemaphoreType.DMA((owners,)),
            pltpu.SemaphoreType.DMA((3,)),
            pltpu.SemaphoreType.DMA((n_hot,)),
            pltpu.SemaphoreType.DMA((n_hot,)),
        ],
        compiler_params=pltpu.CompilerParams(
            collective_id=0, has_side_effects=True, vmem_limit_bytes=63 * 1024 * 1024 - 1536 * 1024
        ),
    )(ids, hot_grads, slots, cold_grads.reshape(owners, capacity, width))
    return hot, cold.reshape(1, OWN_ROWS, width)


def solution(mesh):
    body = functools.partial(per_device, mesh.shape["gx"], mesh.shape["gy"])
    return jax.shard_map(
        body,
        mesh=mesh,
        in_specs=(
            P(("gx", "gy")),
            P(("gx", "gy"), None),
            P("gx", "gy", None, None, None),
            P("gx", "gy", None, None),
            P("gx", "gy", None),
        ),
        out_specs=(P(), P("gx", "gy", None)),
        check_vma=False,
    )
```

profile of v0, /device:TPU:0, one launch (start us, length us, event | category | flops | bytes accessed | tf_op | source)
XLA Modules:
  0.0 55.8 jit_solution(6939670761675025125)
XLA Ops:
  0.6 0.7 %reshape.35 = s32[8,4,128]{2,1,0:T(4,128)S(1)} reshape(s32[1,1,8,512]{3,2,1,0:T(8,128)} %param.8) | data formatting | bytes 32768 | tf_op jit(solution)/shard_map/reshape | solution.py:228
  1.4 0.7 %compare_select_fusion = s32[8,4,128]{2,1,0:T(4,128)S(1)} fusion(s32[8,4,128]{2,1,0:T(4,128)S(1)} %reshape.35, s32[4,128]{1,0:T(4,128)S(1)} %multiply_add_fusion, s32[8]{0:T(128)} %bitcast.9), kind=kLoop, calls=%fused_computation | loop fusion | flops 8192 | bytes 34848 | tf_op jit(solution)/shard_map/jit(_where)/select_n | solution.py:228
  2.1 0.6 %pad.4.slots_ref = s32[8,8,128]{2,1,0:T(8,128)} pad(s32[8,4,128]{2,1,0:T(4,128)S(1)} %compare_select_fusion, s32[]{:T(128)} %constant.3.clone.1), padding=0_0x0_4x0_0 | pad | bytes 49156 | tf_op jit(solution)/shard_map/jit(_pad)/pad | solution.py:232
  2.7 49.8 %shard_map.68 = (f32[2048,128]{1,0:T(8,128)}, f32[2048,128]{1,0:T(8,128)}) custom-call(s32[8,8,128]{2,1,0:T(8,128)} %bitcast.8, bf16[8192,128]{1,0:T(8,128)(2,1)} %hot_ref.1, s32[8,8,128]{2,1,0:T(8,128)} %pad.4.slots_ref, bf16[8,512,128]{2,1,0:T(8,128)(2,1)} %bitcast.6), custom_call_target="tpu_custom_call" | custom-call | tf_op jit(solution)/shard_map/pallas_call | solution.py:245
  52.5 0.0 copy-start
  52.5 2.4 %copy.9 = f32[2048,128]{1,0:T(8,128)} copy(f32[2048,128]{1,0:T(8,128)} %get-tuple-element.8) | data formatting | bytes 2097152
  54.9 0.0 copy-done
  54.9 1.0 %copy.10 = f32[1,2048,128]{2,1,0:T(8,128)} copy(f32[1,2048,128]{2,1,0:T(8,128)S(1)} %bitcast.7) | data formatting | bytes 2097152
  (1 shorter events, 0.0 us)
Async XLA Ops:
  52.5 2.4 %copy-start = (f32[2048,128]{1,0:T(8,128)S(1)}, f32[2048,128]{1,0:T(8,128)}, u32[]{:S(2)}) copy-start(f32[2048,128]{1,0:T(8,128)} %get-tuple-element.5) | copy-start | bytes 3145732
where the time goes:
time: 56.1 us; the launch traced here: 55.8 us
  Pallas kernels  49.8 us (89%)
  local copies, waits for them, and re-layouts  4.68 us (8%)
  other arithmetic  0.73 us (1%)
  between operations  0.65 us (1%)
    pallas_call x1, Pallas kernels, per_device(): pl.pallas_call(functools.partial(kernel, nx, ny, factor, cap_pieces), out...  49.8 us
    unnamed x4, local copies, waits for them, and re-layouts  3.32 us

commit v1 on v0

v1 whole, which is shorter than its diff:
```python
import functools

import jax
import jax.numpy as jnp
from jax import lax
from jax.experimental import pallas as pl
from jax.experimental.pallas import tpu as pltpu
from jax.sharding import PartitionSpec as P

HOT = 2048
OWN_ROWS = 2048
LANES = 128
HIGH = 4
KBLOCK = 4096
MESH = pl.DeviceIdType.MESH
bf16, f32, i16 = jnp.bfloat16, jnp.float32, jnp.int16


def bits(n):
    assert n & (n - 1) == 0
    return n.bit_length() - 1


def one_hot(row, size):
    places = lax.broadcasted_iota(jnp.int32, (size, LANES), 0).astype(i16)
    return jnp.where(places == jnp.concatenate([row] * (size // 16), axis=0), bf16(1), bf16(0))


def spread(codes, data, wanted):
    return jnp.concatenate(
        [jnp.where(codes == i16(w), data, jnp.zeros_like(data)) for w in wanted], axis=1
    )


def kernel(
    nx, ny, factor, waves,
    ids_ref, hot_ref, slots_ref, counts_ref, cold_ref, hot_out, cold_out,
    hotv, idsv, codes, lows, slotv, sstage, crecv, srecv, tab, mine, give, take,
    l1a, l1b, l2a, l2b, l3a, l3b,
    local_sem, csend, crsem, ssend, srsem, hsend, hrecv,
):
    gx, gy = lax.axis_index("gx"), lax.axis_index("gy")
    px, py = 2, 2
    nxr, nyr = nx // px, ny // py
    cc, xx = lax.rem(gx, px), gx // px
    yy, zz = lax.rem(gy, py), gy // py
    piece = HOT // (2 * nx * ny)
    chain = HOT // px // 2
    half = chain // 2
    kblocks = hotv.shape[0] // KBLOCK
    cap_pieces = crecv.shape[1] // LANES
    own_low = OWN_ROWS // HIGH

    def at(c, x, y, z):
        return (x * px + c, z * py + y)

    def near_x(j):
        return at(cc, lax.rem(xx + j, nxr), yy, zz)

    def near_y(j):
        return at(cc, xx, lax.rem(yy + j, py), zz)

    def near_z(j):
        return at(cc, xx, yy, lax.rem(zz + j, nyr))

    def plane(dx, dy):
        return at(cc, lax.rem(xx + dx, nxr), lax.rem(yy + dy, py), zz)

    partner = at(1 - cc, xx, yy, zz)

    def cold_peer(t, sign):
        da, db = t // py, t % py
        a = lax.rem(zz + sign * da + nyr, nyr)
        b = lax.rem(yy + sign * db + py, py)
        return a * py + b

    ids_copy = pltpu.make_async_copy(ids_ref, idsv, local_sem.at[0])
    slots_copy = pltpu.make_async_copy(slots_ref, slotv, local_sem.at[1])
    own_copy = pltpu.make_async_copy(cold_ref.at[gy], crecv.at[0], local_sem.at[2])
    hot_copies = [
        pltpu.make_async_copy(
            hot_ref.at[pl.ds(k * KBLOCK, KBLOCK), :], hotv.at[pl.ds(k * KBLOCK, KBLOCK), :], local_sem.at[3 + k]
        )
        for k in range(kblocks)
    ]
    barrier = pltpu.get_barrier_semaphore()
    greet = [partner]
    greet += [plane(dx, dy) for dx in range(nxr) for dy in range(py) if dx + dy > 0]
    greet += [at(cc, xx, t % py, t // py) for t in ()]
    for t in range(1, ny):
        if t >= py:
            greet.append((gx, cold_peer(t, 1)))
    for device in greet:
        pl.semaphore_signal(barrier, inc=1, device_id=device, device_id_type=MESH)
    slots_copy.start()
    ids_copy.start()
    for copy in hot_copies:
        copy.start()

    slots_copy.wait()
    owners = slotv.shape[0]
    sub = lax.broadcasted_iota(jnp.int32, (owners, LANES), 0)
    lane = lax.broadcasted_iota(jnp.int32, (owners, LANES), 1)
    count = jnp.zeros((owners, LANES), jnp.int32)
    for o in range(owners):
        count = jnp.where(sub == o, counts_ref[o], count)
    for j in range(sstage.shape[1]):
        if j < cap_pieces:
            sstage[:, j, :] = jnp.where(lane + j * LANES < count, slotv[:, j * LANES : (j + 1) * LANES], -1)
        else:
            sstage[:, j, :] = jnp.full((owners, LANES), -1, jnp.int32)

    def cold_copies(t):
        peer = cold_peer(t, 1)
        return (
            pltpu.make_async_remote_copy(
                src_ref=cold_ref.at[peer], dst_ref=crecv.at[t],
                send_sem=csend.at[t], recv_sem=crsem.at[t],
                device_id=(gx, peer), device_id_type=MESH,
            ),
            pltpu.make_async_remote_copy(
                src_ref=sstage.at[peer], dst_ref=srecv.at[t],
                send_sem=ssend.at[t], recv_sem=srsem.at[t],
                device_id=(gx, peer), device_id_type=MESH,
            ),
        )

    def cold_start(ts):
        for t in ts:
            for copy in cold_copies(t):
                copy.start()

    def cold_add(ts, first=False):
        selectors, rows = [], []
        for t in ts:
            slots = sstage[gy] if t == 0 else srecv[t]
            low = jnp.bitwise_and(slots, own_low - 1)
            high = (slots >> bits(own_low)).T
            for j in range(cap_pieces):
                selectors.append(one_hot(jnp.broadcast_to(low[j : j + 1, :], (16, LANES)).astype(i16), own_low))
                code = jnp.broadcast_to(high[:, j : j + 1], (LANES, LANES)).astype(i16)
                rows.append(spread(code, crecv[t, j * LANES : (j + 1) * LANES, :], range(HIGH)))
        total = jnp.dot(
            jnp.concatenate(selectors, axis=1), jnp.concatenate(rows, axis=0), preferred_element_type=f32
        )
        for h in range(HIGH):
            part = total[:, h * LANES : (h + 1) * LANES]
            place = slice(h * own_low, (h + 1) * own_low)
            if first:
                cold_out[place, :] = part
            else:
                cold_out[place, :] += part

    def cold_take(ts):
        for t in ts:
            for copy in cold_copies(t):
                copy.wait()
        cold_add(ts)

    def split_ids(ids):
        row = ids & (piece - 1)
        rest = ids >> bits(piece)
        ch = rest & 1
        rest = rest >> 1
        z = ((rest & (nyr - 1)) - zz) & (nyr - 1)
        rest = rest >> bits(nyr)
        y = ((rest & (py - 1)) - yy) & (py - 1)
        rest = rest >> bits(py)
        x = ((rest & (nxr - 1)) - xx) & (nxr - 1)
        core = ((rest >> bits(nxr)) - cc) & 1
        top = jnp.where(ch == 0, x * py + y, y * nxr + x)
        place = (top * nyr + z) * piece + row
        return ch * half + (place & (half - 1)), core * 2 + (place >> bits(half))

    def hot_block(p, k):
        pieces = KBLOCK // LANES
        selectors, rows = [], []
        for q in range(pieces // 8):
            if p == 0:
                low, code = split_ids(idsv[k * pieces // 8 + q])
                columns = code.T
            for j in range(8):
                i = k * pieces + q * 8 + j
                here = slice(i * LANES, (i + 1) * LANES)
                if p == 0:
                    low_row = jnp.broadcast_to(low[j : j + 1, :], (16, LANES)).astype(i16)
                    column = jnp.broadcast_to(columns[:, j : j + 1], (LANES, LANES)).astype(i16)
                    lows[i] = low_row
                    codes[here, :] = column
                else:
                    low_row = lows[i]
                    column = codes[here, :]
                selectors.append(one_hot(low_row, chain))
                rows.append(spread(column, hotv[here, :], (1 - p, 3 - p)))
        total = jnp.dot(
            jnp.concatenate(selectors, axis=1), jnp.concatenate(rows, axis=0), preferred_element_type=f32
        )
        where = slice((1 - p) * half, (2 - p) * half)
        for c in range(2):
            part = total[c * half : (c + 1) * half, :LANES]
            if k == 0:
                tab[c, where, :] = part
            else:
                tab[c, where, :] += part
        if k == 0:
            give[p] = total[:, LANES:]
        else:
            give[p] += total[:, LANES:]

    used = [0]
    sent = []

    def send(src, dst, device):
        copy = pltpu.make_async_remote_copy(
            src_ref=src, dst_ref=dst, send_sem=hsend.at[used[0]], recv_sem=hrecv.at[used[0]],
            device_id=device, device_id_type=MESH,
        )
        used[0] += 1
        copy.start()
        sent.append(copy)
        return copy

    def arrival(ref, index):
        return pltpu.make_async_remote_copy(
            src_ref=ref, dst_ref=ref, send_sem=hsend.at[index], recv_sem=hrecv.at[index],
            device_id=partner, device_id_type=MESH,
        )

    stage1 = [(nxr, near_x, l1a), (py, near_y, l1b)]
    stage2 = [(py, near_y, l2a), (nxr, near_x, l2b)]
    stage3 = [(nyr, near_z, l3a), (nyr, near_z, l3b)]

    def stage1_sends(js):
        copies = {}
        for early in (True, False):
            for c in range(2):
                n, near, landing = stage1[c]
                size = chain // n
                keep = size // stage2[c][0]
                for j in js(n):
                    lo, hi = (keep, size) if early else (0, keep)
                    copies[early, c, j] = send(
                        tab.at[c, pl.ds(j * size + lo, hi - lo), :],
                        landing.at[j - 1, pl.ds(lo, hi - lo), :], near(j),
                    )
        return copies

    def add_take(p):
        where = slice((1 - p) * half, (2 - p) * half)
        for c in range(2):
            tab[c, where, :] += take[p, c * half : (c + 1) * half, :]

    pl.semaphore_wait(barrier, len(greet))
    cold_start(waves[0])
    own_copy.start()
    ids_copy.wait()
    for k in range(kblocks):
        hot_copies[k].wait()
        hot_block(0, k)
    core0 = send(give.at[0], take.at[0], partner)
    hot_block(1, 0)
    core0.wait_recv()
    add_take(0)
    first = stage1_sends(lambda n: range(n - 1, n // 2 - 1, -1))
    for k in range(1, kblocks):
        hot_block(1, k)
    core1 = send(give.at[1], take.at[1], partner)
    own_copy.wait()
    cold_add([0], first=True)
    core1.wait_recv()
    add_take(1)
    first.update(stage1_sends(lambda n: range(n // 2 - 1, 0, -1)))
    second = {}
    for early in (True, False):
        for c in range(2):
            n, _, landing = stage1[c]
            size = chain // n
            keep = size // stage2[c][0]
            lo, hi = (keep, size) if early else (0, keep)
            for j in range(1, n):
                first[early, c, j].wait_recv()
            for j in range(1, n):
                tab[c, lo:hi, :] += landing[j - 1, lo:hi, :]
            if early:
                n2, near, landing2 = stage2[c]
                for j in range(1, n2):
                    second[c, j] = send(tab.at[c, pl.ds(j * keep, keep), :], landing2.at[j - 1], near(j))
    third = {}
    for c in range(2):
        n, _, landing = stage2[c]
        size = chain // stage1[c][0] // n
        for j in range(1, n):
            second[c, j].wait_recv()
        for j in range(1, n):
            tab[c, :size, :] += landing[j - 1]
        n3, near, landing3 = stage3[c]
        for j in range(1, n3):
            third[c, j] = send(tab.at[c, pl.ds(j * piece, piece), :], landing3.at[j - 1], near(j))
    cold_start(waves[1])
    for group in waves[3]:
        cold_take(group)

    def block(c, x, y, z):
        index = ((c * nxr + x) * py + y) * nyr + z
        return pl.ds(pl.multiple_of(index * 2 * piece, 2 * piece), 2 * piece)

    base = (((cc * nxr + xx) * py + yy) * nyr + zz) * 2 * piece
    for c in range(2):
        n3, _, landing3 = stage3[c]
        for j in range(1, n3):
            third[c, j].wait_recv()
        total = tab[c, :piece, :]
        for j in range(1, n3):
            total = total + landing3[j - 1]
        hot_out[pl.ds(pl.multiple_of(base + c * piece, 8), piece), :] = total * factor

    def out(rows):
        return hot_out.at[rows, :]

    own = out(block(cc, xx, yy, zz))
    z_index = used[0]
    for j in range(1, nyr):
        send(own, own, near_z(j))
    plane_steps = [(dx, dy) for dx in range(nxr) for dy in range(py) if dx + dy > 0]
    plane_index, core_index = {}, {}

    def pass_on(j):
        rows = out(block(cc, xx, yy, lax.rem(zz + j, nyr)))
        for dx, dy in plane_steps:
            plane_index[dx, dy, j] = used[0]
            send(rows, rows, plane(dx, dy))
        core_index[0, 0, j] = used[0]
        send(rows, rows, partner)

    pass_on(0)
    cold_start(waves[2])
    order = sorted(range(1, nyr), key=lambda j: min(j, nyr - j))
    for j in order:
        rows = out(block(cc, xx, yy, lax.rem(zz + j, nyr)))
        arrival(rows, z_index + nyr - j - 1).wait_recv()
        pass_on(j)
    for group in waves[4]:
        cold_take(group)
    for j in [0] + order:
        for dx, dy in plane_steps:
            rows = out(block(cc, lax.rem(xx - dx + nxr, nxr), lax.rem(yy - dy + py, py), lax.rem(zz + j, nyr)))
            arrival(rows, plane_index[dx, dy, j]).wait_recv()
            core_index[dx, dy, j] = used[0]
            send(rows, rows, partner)
    for group in waves[5]:
        cold_take(group)
    for (dx, dy, j), index in core_index.items():
        rows = out(block(1 - cc, lax.rem(xx - dx + nxr, nxr), lax.rem(yy - dy + py, py), lax.rem(zz + j, nyr)))
        arrival(rows, index).wait_recv()
    for copy in sent:
        copy.wait_send()


def make_waves(ny, py):
    every = list(range(1, ny))
    if ny != 8:
        return [every[: ny // 2], [], every[ny // 2 :], [[t] for t in every[: ny // 2]], [], [[t] for t in every[ny // 2 :]]]
    return [[4, 2, 6], [], [5, 3, 7, 1], [[4, 2], [6]], [], [[5, 3], [7, 1]]]


def per_device(nx, ny, hot_ids, hot_grads, cold_grads, cold_slots, cold_counts):
    look, width = hot_grads.shape
    owners, capacity = cold_slots.shape[2], cold_slots.shape[3]
    px, py = 2, 2
    nxr, nyr = nx // px, ny // py
    factor = (HOT / (look * nx * ny)) ** 0.5
    chain = HOT // px // 2
    piece = chain // (nxr * ny)
    cap_pieces = capacity // LANES
    ids = hot_ids.reshape(-1, 8, LANES)
    n_sends = 2 + 4 * (nxr - 1) + 2 + 4 * (py - 1) + 3 * nyr + nxr * py * nyr * 2 + 8
    hbm = pl.BlockSpec(memory_space=pltpu.HBM)
    vmem = pl.BlockSpec(memory_space=pltpu.VMEM)
    smem = pl.BlockSpec(memory_space=pltpu.SMEM)
    dma = pltpu.SemaphoreType.DMA
    hot, cold = pl.pallas_call(
        functools.partial(kernel, nx, ny, factor, make_waves(ny, py)),
        out_shape=(
            jax.ShapeDtypeStruct((HOT, width), f32),
            jax.ShapeDtypeStruct((OWN_ROWS, width), f32),
        ),
        in_specs=[hbm, hbm, hbm, smem, hbm],
        out_specs=(vmem, vmem),
        scratch_shapes=[
            pltpu.VMEM((look, width), bf16),
            pltpu.VMEM(ids.shape, jnp.int32),
            pltpu.VMEM((look, LANES), i16),
            pltpu.VMEM((look // LANES, 16, LANES), i16),
            pltpu.VMEM((owners, capacity), jnp.int32),
            pltpu.VMEM((owners, -(-cap_pieces // 8) * 8, LANES), jnp.int32),
            pltpu.VMEM((owners, capacity, width), bf16),
            pltpu.VMEM((owners, -(-cap_pieces // 8) * 8, LANES), jnp.int32),
            pltpu.VMEM((2, chain, width), f32),
            pltpu.VMEM((8, width), f32),
            pltpu.VMEM((2, chain, width), f32),
            pltpu.VMEM((2, chain, width), f32),
            pltpu.VMEM((nxr - 1, chain // nxr, width), f32),
            pltpu.VMEM((py - 1, chain // py, width), f32),
            pltpu.VMEM((py - 1, chain // nxr // py, width), f32),
            pltpu.VMEM((nxr - 1, chain // nxr // py, width), f32),
            pltpu.VMEM((nyr - 1, piece, width), f32),
            pltpu.VMEM((nyr - 1, piece, width), f32),
            dma((3 + look // KBLOCK,)),
            dma((owners,)),
            dma((owners,)),
            dma((owners,)),
            dma((owners,)),
            dma((n_sends,)),
            dma((n_sends,)),
        ],
        compiler_params=pltpu.CompilerParams(
            collective_id=0, has_side_effects=True, vmem_limit_bytes=VMEM_KIB * 1024
        ),
    )(*(
        pltpu.with_memory_space_constraint(x, pltpu.HBM)
        for x in (ids, hot_grads, cold_slots.reshape(owners, capacity), cold_counts.reshape(owners), cold_grads.reshape(owners, capacity, width))
    ))
    return hot, cold.reshape(1, OWN_ROWS, width)


VMEM_KIB = 40000


def solution(mesh):
    body = functools.partial(per_device, mesh.shape["gx"], mesh.shape["gy"])
    return jax.shard_map(
        body,
        mesh=mesh,
        in_specs=(
            P(("gx", "gy")),
            P(("gx", "gy"), None),
            P("gx", "gy", None, None, None),
            P("gx", "gy", None, None),
            P("gx", "gy", None),
        ),
        out_specs=(P(), P("gx", "gy", None)),
        check_vma=False,
    )
```

time: 56.1 us -> 49.8 us (0.89)
  Pallas kernels: 49.8 us -> 47 us
  local copies, waits for them, and re-layouts: 4.68 us -> 1.94 us
  other arithmetic: 0.73 us -> 0 us
    pallas_call x1, Pallas kernels: 49.8 us -> 47 us  [per_device(): pl.pallas_call(functools.partial(kernel, nx, ny, factor, make_waves(ny, p...]
    unnamed x4 -> x2, local copies, waits for them, and re-layouts: 3.32 us -> 1.94 us
    reshape x1 -> x0, local copies, waits for them, and re-layouts: 0.73 us -> none  [per_device(): cold_slots.reshape(owners, capacity)]
    select_n x1 -> x0, other arithmetic: 0.73 us -> none  [per_device(): jnp.where(places < cold_counts.reshape(owners, 1), cold_slots.reshape(own...]
    pad x1 -> x0, local copies, waits for them, and re-layouts: 0.62 us -> none  [per_device(): slots = jnp.pad(slots, ((0, 0), (0, pad), (0, 0)), constant_values=-1)]
where the time goes in v1:
time: 49.8 us; the launch traced here: 49.6 us
  Pallas kernels  47 us (94%)
  local copies, waits for them, and re-layouts  1.94 us (4%)
  between operations  0.64 us (1%)
    pallas_call x1, Pallas kernels, per_device(): pl.pallas_call(functools.partial(kernel, nx, ny, factor, make_waves(ny, p...  47 us
    unnamed x2, local copies, waits for them, and re-layouts  1.94 us

profile of v1, /device:TPU:0, one launch (start us, length us, event | category | flops | bytes accessed | tf_op | source)
XLA Modules:
  0.0 49.6 jit_solution(8486379199199208899)
XLA Ops:
  0.6 47.0 %shard_map.68 = (f32[2048,128]{1,0:T(8,128)S(1)}, f32[2048,128]{1,0:T(8,128)S(1)}) custom-call(s32[8,8,128]{2,1,0:T(8,128)} %bitcast.7, bf16[8192,128]{1,0:T(8,128)(2,1)} %hot_ref.1, s32[8,512]{1,0:T(8,128)} %bitcast.8, s32[8]{0:T(128)} %bitcast.9, bf16[8,512,128]{2,1,0:T(8,128)(2,1)} %bitcast.6), custom_call_target="tpu_custom_call" | custom-call | tf_op jit(solution)/shard_map/pallas_call | solution.py:381
  47.7 1.0 %copy.9 = f32[2048,128]{1,0:T(8,128)} copy(f32[2048,128]{1,0:T(8,128)S(1)} %get-tuple-element.8) | data formatting | bytes 2097152
  48.6 1.0 %copy.10 = f32[1,2048,128]{2,1,0:T(8,128)} copy(f32[1,2048,128]{2,1,0:T(8,128)S(1)} %bitcast.5) | data formatting | bytes 2097152

commit v2 on v1

--- a/solution.py
+++ b/solution.py
@@ -33,10 +33,10 @@
 
 
 def kernel(
-    nx, ny, factor, waves,
+    nx, ny, factor, sends, takes,
     ids_ref, hot_ref, slots_ref, counts_ref, cold_ref, hot_out, cold_out,
-    hotv, idsv, codes, lows, slotv, sstage, crecv, srecv, tab, mine, give, take,
-    l1a, l1b, l2a, l2b, l3a, l3b,
+    hotv, idsv, codes, lows, slotv, sstage, crecv, srecv, tab, give, take,
+    l1a, l1b, l2a, l2b, l3a, l3b, coded, scales, counts_smem, fence_sem,
     local_sem, csend, crsem, ssend, srsem, hsend, hrecv,
 ):
     gx, gy = lax.axis_index("gx"), lax.axis_index("gy")
@@ -76,59 +76,48 @@
 
     ids_copy = pltpu.make_async_copy(ids_ref, idsv, local_sem.at[0])
     slots_copy = pltpu.make_async_copy(slots_ref, slotv, local_sem.at[1])
+    counts_copy = pltpu.make_async_copy(counts_ref, counts_smem, local_sem.at[3])
     own_copy = pltpu.make_async_copy(cold_ref.at[gy], crecv.at[0], local_sem.at[2])
     hot_copies = [
         pltpu.make_async_copy(
-            hot_ref.at[pl.ds(k * KBLOCK, KBLOCK), :], hotv.at[pl.ds(k * KBLOCK, KBLOCK), :], local_sem.at[3 + k]
+            hot_ref.at[pl.ds(k * KBLOCK, KBLOCK), :], hotv.at[pl.ds(k * KBLOCK, KBLOCK), :], local_sem.at[4 + k]
         )
         for k in range(kblocks)
     ]
     barrier = pltpu.get_barrier_semaphore()
     greet = [partner]
     greet += [plane(dx, dy) for dx in range(nxr) for dy in range(py) if dx + dy > 0]
-    greet += [at(cc, xx, t % py, t // py) for t in ()]
     for t in range(1, ny):
         if t >= py:
             greet.append((gx, cold_peer(t, 1)))
     for device in greet:
         pl.semaphore_signal(barrier, inc=1, device_id=device, device_id_type=MESH)
+    counts_copy.start()
     slots_copy.start()
     ids_copy.start()
     for copy in hot_copies:
         copy.start()
-
-    slots_copy.wait()
-    owners = slotv.shape[0]
-    sub = lax.broadcasted_iota(jnp.int32, (owners, LANES), 0)
-    lane = lax.broadcasted_iota(jnp.int32, (owners, LANES), 1)
-    count = jnp.zeros((owners, LANES), jnp.int32)
-    for o in range(owners):
-        count = jnp.where(sub == o, counts_ref[o], count)
-    for j in range(sstage.shape[1]):
-        if j < cap_pieces:
-            sstage[:, j, :] = jnp.where(lane + j * LANES < count, slotv[:, j * LANES : (j + 1) * LANES], -1)
-        else:
-            sstage[:, j, :] = jnp.full((owners, LANES), -1, jnp.int32)
-
-    def cold_copies(t):
+    pl.semaphore_wait(barrier, len(greet))
+
+    def cold_copy(t, part):
         peer = cold_peer(t, 1)
-        return (
-            pltpu.make_async_remote_copy(
-                src_ref=cold_ref.at[peer], dst_ref=crecv.at[t],
-                send_sem=csend.at[t], recv_sem=crsem.at[t],
-                device_id=(gx, peer), device_id_type=MESH,
-            ),
-            pltpu.make_async_remote_copy(
-                src_ref=sstage.at[peer], dst_ref=srecv.at[t],
-                send_sem=ssend.at[t], recv_sem=srsem.at[t],
-                device_id=(gx, peer), device_id_type=MESH,
-            ),
-        )
-
-    def cold_start(ts):
-        for t in ts:
-            for copy in cold_copies(t):
-                copy.start()
+        source, landing, send_sem, recv_sem = (
+            (cold_ref, crecv, csend, crsem) if part == 0 else (sstage, srecv, ssend, srsem)
+        )
+        return pltpu.make_async_remote_copy(
+            src_ref=source.at[peer], dst_ref=landing.at[t],
+            send_sem=send_sem.at[t], recv_sem=recv_sem.at[t],
+            device_id=(gx, peer), device_id_type=MESH,
+        )
+
+    def cold_start(ts, parts=(1, 0)):
+        for part in parts:
+            for t in ts:
+                cold_copy(t, part).start()
+
+    def fence():
+        pl.semaphore_signal(fence_sem, 1)
+        pl.semaphore_wait(fence_sem, 1)
 
     def cold_add(ts, first=False):
         selectors, rows = [], []
@@ -153,8 +142,8 @@
 
     def cold_take(ts):
         for t in ts:
-            for copy in cold_copies(t):
-                copy.wait()
+            for part in range(2):
+                cold_copy(t, part).wait()
         cold_add(ts)
 
     def split_ids(ids):
@@ -250,21 +239,41 @@
         for c in range(2):
             tab[c, where, :] += take[p, c * half : (c + 1) * half, :]
 
-    pl.semaphore_wait(barrier, len(greet))
-    cold_start(waves[0])
+    cold_start(sends[0], (0,))
     own_copy.start()
+    counts_copy.wait()
+    slots_copy.wait()
+    owners = slotv.shape[0]
+    sub = lax.broadcasted_iota(jnp.int32, (owners, LANES), 0)
+    lane = lax.broadcasted_iota(jnp.int32, (owners, LANES), 1)
+    count = jnp.zeros((owners, LANES), jnp.int32)
+    for o in range(owners):
+        count = jnp.where(sub == o, counts_smem[o], count)
+    for j in range(sstage.shape[1]):
+        if j < cap_pieces:
+            sstage[:, j, :] = jnp.where(lane + j * LANES < count, slotv[:, j * LANES : (j + 1) * LANES], -1)
+        else:
+            sstage[:, j, :] = jnp.full((owners, LANES), -1, jnp.int32)
+
+    cold_start(sends[0], (1,))
     ids_copy.wait()
     for k in range(kblocks):
         hot_copies[k].wait()
         hot_block(0, k)
     core0 = send(give.at[0], take.at[0], partner)
+    cold_start(sends[1])
+    fence()
     hot_block(1, 0)
     core0.wait_recv()
     add_take(0)
     first = stage1_sends(lambda n: range(n - 1, n // 2 - 1, -1))
+    cold_start(sends[2])
+    fence()
     for k in range(1, kblocks):
         hot_block(1, k)
     core1 = send(give.at[1], take.at[1], partner)
+    cold_start(sends[3])
+    fence()
     own_copy.wait()
     cold_add([0], first=True)
     core1.wait_recv()
@@ -285,6 +294,7 @@
                 n2, near, landing2 = stage2[c]
                 for j in range(1, n2):
                     second[c, j] = send(tab.at[c, pl.ds(j * keep, keep), :], landing2.at[j - 1], near(j))
+    cold_start(sends[4])
     third = {}
     for c in range(2):
         n, _, landing = stage2[c]
@@ -296,15 +306,21 @@
         n3, near, landing3 = stage3[c]
         for j in range(1, n3):
             third[c, j] = send(tab.at[c, pl.ds(j * piece, piece), :], landing3.at[j - 1], near(j))
-    cold_start(waves[1])
-    for group in waves[3]:
+    cold_start(sends[5])
+    for group in takes[0]:
         cold_take(group)
 
     def block(c, x, y, z):
-        index = ((c * nxr + x) * py + y) * nyr + z
-        return pl.ds(pl.multiple_of(index * 2 * piece, 2 * piece), 2 * piece)
-
-    base = (((cc * nxr + xx) * py + yy) * nyr + zz) * 2 * piece
+        return ((c * nxr + x) * py + y) * nyr + z
+
+    rows = 2 * piece
+    groups = rows // 8
+    eye = [
+        lax.broadcasted_iota(jnp.int32, (8, LANES), 1)
+        == lax.broadcasted_iota(jnp.int32, (8, LANES), 0) + g * 8
+        for g in range(groups)
+    ]
+    totals = []
     for c in range(2):
         n3, _, landing3 = stage3[c]
         for j in range(1, n3):
@@ -312,55 +328,91 @@
         total = tab[c, :piece, :]
         for j in range(1, n3):
             total = total + landing3[j - 1]
-        hot_out[pl.ds(pl.multiple_of(base + c * piece, 8), piece), :] = total * factor
-
-    def out(rows):
-        return hot_out.at[rows, :]
-
-    own = out(block(cc, xx, yy, zz))
-    z_index = used[0]
-    for j in range(1, nyr):
-        send(own, own, near_z(j))
+        totals.append(total)
+    total = jnp.concatenate(totals, axis=0) * factor
+    largest = jnp.max(jnp.abs(total), axis=1, keepdims=True)
+    unit = jnp.where(largest > 0, 32767.0 / largest, 0.0)
+    steps = jnp.round(jnp.clip(total * unit, -32767.0, 32767.0)).astype(jnp.int32).astype(i16)
+    mine = block(cc, xx, yy, zz)
+    coded[mine] = steps
+    size = jnp.broadcast_to(largest * (1.0 / 32767.0), (rows, LANES))
+    row = jnp.zeros((8, LANES), f32)
+    for g in range(groups):
+        row = row + jnp.where(eye[g], size[g * 8 : (g + 1) * 8, :], 0.0)
+    scales[mine] = jnp.sum(row, axis=0, keepdims=True)
+
+    def decode(index):
+        row = jnp.broadcast_to(scales[index], (8, LANES))
+        value = coded[index].astype(jnp.int32).astype(f32)
+        for g in range(groups):
+            size = jnp.sum(jnp.where(eye[g], row, 0.0), axis=1, keepdims=True)
+            hot_out[pl.ds(pl.multiple_of(index * rows + g * 8, 8), 8), :] = value[g * 8 : (g + 1) * 8, :] * size
+
+    def share(place, device):
+        index = used[0]
+        for ref in (scales, coded):
+            send(ref.at[place], ref.at[place], device)
+        return index
+
+    def arrived(place, index):
+        for n, ref in enumerate((scales, coded)):
+            arrival(ref.at[place], index + n).wait_recv()
+
+    z_index = {j: share(mine, near_z(j)) for j in range(1, nyr)}
     plane_steps = [(dx, dy) for dx in range(nxr) for dy in range(py) if dx + dy > 0]
     plane_index, core_index = {}, {}
 
+    def column(c, x, y):
+        return pl.ds(block(c, x, y, 0), nyr)
+
+    def from_plane(dx, dy):
+        return lax.rem(xx - dx + nxr, nxr), lax.rem(yy - dy + py, py)
+
     def pass_on(j):
-        rows = out(block(cc, xx, yy, lax.rem(zz + j, nyr)))
         for dx, dy in plane_steps:
-            plane_index[dx, dy, j] = used[0]
-            send(rows, rows, plane(dx, dy))
-        core_index[0, 0, j] = used[0]
-        send(rows, rows, partner)
-
+            plane_index[dx, dy, j] = share(block(cc, xx, yy, lax.rem(zz + j, nyr)), plane(dx, dy))
+
+    cold_start(sends[6])
     pass_on(0)
-    cold_start(waves[2])
+    cold_start(sends[7])
     order = sorted(range(1, nyr), key=lambda j: min(j, nyr - j))
     for j in order:
-        rows = out(block(cc, xx, yy, lax.rem(zz + j, nyr)))
-        arrival(rows, z_index + nyr - j - 1).wait_recv()
+        arrived(block(cc, xx, yy, lax.rem(zz + j, nyr)), z_index[nyr - j])
         pass_on(j)
-    for group in waves[4]:
+    core_index[0, 0] = share(column(cc, xx, yy), partner)
+    cold_start(sends[8])
+    for group in takes[1]:
         cold_take(group)
     for j in [0] + order:
-        for dx, dy in plane_steps:
-            rows = out(block(cc, lax.rem(xx - dx + nxr, nxr), lax.rem(yy - dy + py, py), lax.rem(zz + j, nyr)))
-            arrival(rows, plane_index[dx, dy, j]).wait_recv()
-            core_index[dx, dy, j] = used[0]
-            send(rows, rows, partner)
-    for group in waves[5]:
+        decode(block(cc, xx, yy, lax.rem(zz + j, nyr)))
+    for dx, dy in plane_steps:
+        x, y = from_plane(dx, dy)
+        for j in [0] + order:
+            arrived(block(cc, x, y, lax.rem(zz + j, nyr)), plane_index[dx, dy, j])
+        core_index[dx, dy] = share(column(cc, x, y), partner)
+        for z in range(nyr):
+            decode(block(cc, x, y, z))
+    for group in takes[2]:
         cold_take(group)
-    for (dx, dy, j), index in core_index.items():
-        rows = out(block(1 - cc, lax.rem(xx - dx + nxr, nxr), lax.rem(yy - dy + py, py), lax.rem(zz + j, nyr)))
-        arrival(rows, index).wait_recv()
+    for (dx, dy), index in core_index.items():
+        x, y = from_plane(dx, dy)
+        arrived(column(1 - cc, x, y), index)
+        for z in range(nyr):
+            decode(block(1 - cc, x, y, z))
     for copy in sent:
         copy.wait_send()
 
 
-def make_waves(ny, py):
+def make_waves(ny):
+    if ny == 8:
+        return SENDS, TAKES
     every = list(range(1, ny))
-    if ny != 8:
-        return [every[: ny // 2], [], every[ny // 2 :], [[t] for t in every[: ny // 2]], [], [[t] for t in every[ny // 2 :]]]
-    return [[4, 2, 6], [], [5, 3, 7, 1], [[4, 2], [6]], [], [[5, 3], [7, 1]]]
+    early, late = every[: ny // 2], every[ny // 2 :]
+    return [early, [], [], [], [], [], [], late, []], [[[t] for t in early], [], [[t] for t in late]]
+
+
+SENDS = [[5, 3, 1], [], [], [4], [], [], [], [2, 6, 7], []]
+TAKES = [[[5, 3]], [], [[4, 1], [7, 2], [6]]]
 
 
 def per_device(nx, ny, hot_ids, hot_grads, cold_grads, cold_slots, cold_counts):
@@ -373,18 +425,17 @@
     piece = chain // (nxr * ny)
     cap_pieces = capacity // LANES
     ids = hot_ids.reshape(-1, 8, LANES)
-    n_sends = 2 + 4 * (nxr - 1) + 2 + 4 * (py - 1) + 3 * nyr + nxr * py * nyr * 2 + 8
+    n_sends = 2 + 3 * (nxr - 1) + 3 * (py - 1) + 4 * (nyr - 1) + 2 * (nxr * py - 1) * nyr + 2 * nxr * py
     hbm = pl.BlockSpec(memory_space=pltpu.HBM)
     vmem = pl.BlockSpec(memory_space=pltpu.VMEM)
-    smem = pl.BlockSpec(memory_space=pltpu.SMEM)
     dma = pltpu.SemaphoreType.DMA
     hot, cold = pl.pallas_call(
-        functools.partial(kernel, nx, ny, factor, make_waves(ny, py)),
+        functools.partial(kernel, nx, ny, factor, *make_waves(ny)),
         out_shape=(
             jax.ShapeDtypeStruct((HOT, width), f32),
             jax.ShapeDtypeStruct((OWN_ROWS, width), f32),
         ),
-        in_specs=[hbm, hbm, hbm, smem, hbm],
+        in_specs=[hbm, hbm, hbm, hbm, hbm],
         out_specs=(vmem, vmem),
         scratch_shapes=[
             pltpu.VMEM((look, width), bf16),
@@ -396,7 +447,6 @@
             pltpu.VMEM((owners, capacity, width), bf16),
             pltpu.VMEM((owners, -(-cap_pieces // 8) * 8, LANES), jnp.int32),
             pltpu.VMEM((2, chain, width), f32),
-            pltpu.VMEM((8, width), f32),
             pltpu.VMEM((2, chain, width), f32),
             pltpu.VMEM((2, chain, width), f32),
             pltpu.VMEM((nxr - 1, chain // nxr, width), f32),
@@ -405,7 +455,11 @@
             pltpu.VMEM((nxr - 1, chain // nxr // py, width), f32),
             pltpu.VMEM((nyr - 1, piece, width), f32),
             pltpu.VMEM((nyr - 1, piece, width), f32),
-            dma((3 + look // KBLOCK,)),
+            pltpu.VMEM((nx * ny, 2 * piece, width), i16),
+            pltpu.VMEM((nx * ny, 1, LANES), f32),
+            pltpu.SMEM((owners,), jnp.int32),
+            pltpu.SemaphoreType.REGULAR,
+            dma((4 + look // KBLOCK,)),
             dma((owners,)),
             dma((owners,)),
             dma((owners,)),

time: 49.8 us -> 42.1 us (0.85)
  Pallas kernels: 47 us -> 39.4 us
    pallas_call x1, Pallas kernels: 47 us -> 39.4 us  [per_device(): pl.pallas_call(functools.partial(kernel, nx, ny, factor, *make_waves(ny))...]
where the time goes in v2:
time: 42.1 us; the launch traced here: 42 us
  Pallas kernels  39.4 us (94%)
  local copies, waits for them, and re-layouts  1.94 us (5%)
  between operations  0.64 us (2%)
    pallas_call x1, Pallas kernels, per_device(): pl.pallas_call(functools.partial(kernel, nx, ny, factor, *make_waves(ny))...  39.4 us
    unnamed x2, local copies, waits for them, and re-layouts  1.94 us

profile of v2, /device:TPU:0, one launch (start us, length us, event | category | flops | bytes accessed | tf_op | source)
XLA Modules:
  0.0 42.0 jit_solution(13062965996120676405)
XLA Ops:
  0.6 39.4 %shard_map.68 = (f32[2048,128]{1,0:T(8,128)S(1)}, f32[2048,128]{1,0:T(8,128)S(1)}) custom-call(s32[8,8,128]{2,1,0:T(8,128)} %bitcast.7, bf16[8192,128]{1,0:T(8,128)(2,1)} %hot_ref.1, s32[8,512]{1,0:T(8,128)} %bitcast.8, s32[8]{0:T(128)} %bitcast.9, bf16[8,512,128]{2,1,0:T(8,128)(2,1)} %bitcast.6), custom_call_target="tpu_custom_call" | custom-call | tf_op jit(solution)/shard_map/pallas_call | solution.py:432
  40.0 1.0 %copy.9 = f32[2048,128]{1,0:T(8,128)} copy(f32[2048,128]{1,0:T(8,128)S(1)} %get-tuple-element.8) | data formatting | bytes 2097152
  41.0 1.0 %copy.10 = f32[1,2048,128]{2,1,0:T(8,128)} copy(f32[1,2048,128]{2,1,0:T(8,128)S(1)} %bitcast.5) | data formatting | bytes 2097152

commit v3 on v2

--- a/solution.py
+++ b/solution.py
@@ -37,7 +37,7 @@
     ids_ref, hot_ref, slots_ref, counts_ref, cold_ref, hot_out, cold_out,
     hotv, idsv, codes, lows, slotv, sstage, crecv, srecv, tab, give, take,
     l1a, l1b, l2a, l2b, l3a, l3b, coded, scales, counts_smem, fence_sem,
-    local_sem, csend, crsem, ssend, srsem, hsend, hrecv,
+    local_sem, csend, crsem, hsend, hrecv,
 ):
     gx, gy = lax.axis_index("gx"), lax.axis_index("gy")
     px, py = 2, 2
@@ -99,21 +99,27 @@
         copy.start()
     pl.semaphore_wait(barrier, len(greet))
 
+    halves = crecv.shape[1] // 2
+
     def cold_copy(t, part):
         peer = cold_peer(t, 1)
-        source, landing, send_sem, recv_sem = (
-            (cold_ref, crecv, csend, crsem) if part == 0 else (sstage, srecv, ssend, srsem)
-        )
+        if part < 2:
+            rows = pl.ds(part * halves, halves)
+            source, landing = cold_ref.at[peer, rows, :], crecv.at[t, rows, :]
+        else:
+            source, landing = sstage.at[peer], srecv.at[t]
         return pltpu.make_async_remote_copy(
-            src_ref=source.at[peer], dst_ref=landing.at[t],
-            send_sem=send_sem.at[t], recv_sem=recv_sem.at[t],
+            src_ref=source, dst_ref=landing,
+            send_sem=csend.at[3 * t + part], recv_sem=crsem.at[3 * t + part],
             device_id=(gx, peer), device_id_type=MESH,
         )
 
-    def cold_start(ts, parts=(1, 0)):
-        for part in parts:
-            for t in ts:
-                cold_copy(t, part).start()
+    def cold_start(items):
+        for item in items:
+            if item % 2 == 0 and item not in sends[0]:
+                cold_copy(item // 2, 2).start()
+        for item in items:
+            cold_copy(item // 2, item % 2).start()
 
     def fence():
         pl.semaphore_signal(fence_sem, 1)
@@ -142,7 +148,7 @@
 
     def cold_take(ts):
         for t in ts:
-            for part in range(2):
+            for part in range(3):
                 cold_copy(t, part).wait()
         cold_add(ts)
 
@@ -239,7 +245,8 @@
         for c in range(2):
             tab[c, where, :] += take[p, c * half : (c + 1) * half, :]
 
-    cold_start(sends[0], (0,))
+    for item in sends[0]:
+        cold_copy(item // 2, item % 2).start()
     own_copy.start()
     counts_copy.wait()
     slots_copy.wait()
@@ -255,7 +262,9 @@
         else:
             sstage[:, j, :] = jnp.full((owners, LANES), -1, jnp.int32)
 
-    cold_start(sends[0], (1,))
+    for item in sends[0]:
+        if item % 2 == 0:
+            cold_copy(item // 2, 2).start()
     ids_copy.wait()
     for k in range(kblocks):
         hot_copies[k].wait()
@@ -403,16 +412,28 @@
         copy.wait_send()
 
 
+def store(hot_ref, cold_ref, hot_out, cold_out, sem):
+    copies = [
+        pltpu.make_async_copy(hot_ref, hot_out, sem.at[0]),
+        pltpu.make_async_copy(cold_ref, cold_out, sem.at[1]),
+    ]
+    for copy in copies:
+        copy.start()
+    for copy in copies:
+        copy.wait()
+
+
 def make_waves(ny):
     if ny == 8:
         return SENDS, TAKES
     every = list(range(1, ny))
     early, late = every[: ny // 2], every[ny // 2 :]
-    return [early, [], [], [], [], [], [], late, []], [[[t] for t in early], [], [[t] for t in late]]
-
-
-SENDS = [[5, 3, 1], [], [], [4], [], [], [], [2, 6, 7], []]
-TAKES = [[[5, 3]], [], [[4, 1], [7, 2], [6]]]
+    both = lambda ts: [2 * t + h for t in ts for h in range(2)]
+    return [both(early), [], [], [], [], [], [], both(late), []], [[[t] for t in early], [], [[t] for t in late]]
+
+
+SENDS = [[2, 3, 6, 7, 10, 11], [], [], [8, 9], [], [], [], [4, 5, 12, 13, 14, 15], []]
+TAKES = [[[1, 3]], [], [[5, 4], [2, 6], [7]]]
 
 
 def per_device(nx, ny, hot_ids, hot_grads, cold_grads, cold_slots, cold_counts):
@@ -460,10 +481,8 @@
             pltpu.SMEM((owners,), jnp.int32),
             pltpu.SemaphoreType.REGULAR,
             dma((4 + look // KBLOCK,)),
-            dma((owners,)),
-            dma((owners,)),
-            dma((owners,)),
-            dma((owners,)),
+            dma((3 * owners,)),
+            dma((3 * owners,)),
             dma((n_sends,)),
             dma((n_sends,)),
         ],
@@ -474,6 +493,13 @@
         pltpu.with_memory_space_constraint(x, pltpu.HBM)
         for x in (ids, hot_grads, cold_slots.reshape(owners, capacity), cold_counts.reshape(owners), cold_grads.reshape(owners, capacity, width))
     ))
+    hot, cold = pl.pallas_call(
+        store,
+        out_shape=(jax.ShapeDtypeStruct((HOT, width), f32), jax.ShapeDtypeStruct((OWN_ROWS, width), f32)),
+        in_specs=[vmem, vmem],
+        out_specs=(hbm, hbm),
+        scratch_shapes=[dma((2,))],
+    )(*(pltpu.with_memory_space_constraint(x, pltpu.VMEM) for x in (hot, cold)))
     return hot, cold.reshape(1, OWN_ROWS, width)
 
 

time: 42.1 us -> 40.7 us (0.967)
  local copies, waits for them, and re-layouts: 1.94 us -> 0 us
  Pallas kernels: 39.4 us -> 39.9 us
    unnamed x2 -> x0, local copies, waits for them, and re-layouts: 1.94 us -> none
    pallas_call x0 -> x1, Pallas kernels: none -> 1.33 us  [per_device(): pl.pallas_call(store, out_shape=(jax.ShapeDtypeStruct((HOT, width), f32),...]
    pallas_call x1, Pallas kernels: 39.4 us -> 38.5 us  [per_device(): pl.pallas_call(functools.partial(kernel, nx, ny, factor, *make_waves(ny))...]
where the time goes in v3:
time: 40.7 us; the launch traced here: 40.5 us
  Pallas kernels  39.9 us (98%)
  between operations  0.64 us (2%)
    pallas_call x1, Pallas kernels, per_device(): pl.pallas_call(functools.partial(kernel, nx, ny, factor, *make_waves(ny))...  38.5 us
    pallas_call x1, Pallas kernels, per_device(): pl.pallas_call(store, out_shape=(jax.ShapeDtypeStruct((HOT, width), f32),...  1.33 us

profile of v3, /device:TPU:0, one launch (start us, length us, event | category | flops | bytes accessed | tf_op | source)
XLA Modules:
  0.0 40.5 jit_solution(8260193787629873483)
XLA Ops:
  0.6 38.5 %shard_map.68 = (f32[2048,128]{1,0:T(8,128)S(1)}, f32[2048,128]{1,0:T(8,128)S(1)}) custom-call(s32[8,8,128]{2,1,0:T(8,128)} %bitcast.6, bf16[8192,128]{1,0:T(8,128)(2,1)} %hot_ref.1, s32[8,512]{1,0:T(8,128)} %bitcast.7, s32[8]{0:T(128)} %bitcast.8, bf16[8,512,128]{2,1,0:T(8,128)(2,1)} %bitcast.5), custom_call_target="tpu_custom_call" | custom-call | tf_op jit(solution)/shard_map/pallas_call | solution.py:453
  39.2 1.3 %shard_map.69 = (f32[2048,128]{1,0:T(8,128)}, f32[2048,128]{1,0:T(8,128)}) custom-call(f32[2048,128]{1,0:T(8,128)S(1)} %get-tuple-element.6.hot_ref, f32[2048,128]{1,0:T(8,128)S(1)} %get-tuple-element.7.cold_ref), custom_call_target="tpu_custom_call" | custom-call | tf_op jit(solution)/shard_map/pallas_call | solution.py:496

commit v4 on v3

--- a/solution.py
+++ b/solution.py
@@ -401,13 +401,14 @@
         core_index[dx, dy] = share(column(cc, x, y), partner)
         for z in range(nyr):
             decode(block(cc, x, y, z))
-    for group in takes[2]:
+    for group in takes[2][:-1]:
         cold_take(group)
     for (dx, dy), index in core_index.items():
         x, y = from_plane(dx, dy)
         arrived(column(1 - cc, x, y), index)
         for z in range(nyr):
             decode(block(1 - cc, x, y, z))
+    cold_take(takes[2][-1])
     for copy in sent:
         copy.wait_send()
 
@@ -432,8 +433,8 @@
     return [both(early), [], [], [], [], [], [], both(late), []], [[[t] for t in early], [], [[t] for t in late]]
 
 
-SENDS = [[2, 3, 6, 7, 10, 11], [], [], [8, 9], [], [], [], [4, 5, 12, 13, 14, 15], []]
-TAKES = [[[1, 3]], [], [[5, 4], [2, 6], [7]]]
+SENDS = [[6, 7, 2, 3, 10, 11], [], [], [8, 9], [], [], [4, 12], [5, 13, 14, 15], []]
+TAKES = [[[3, 1]], [[5, 4]], [[2, 6], [7]]]
 
 
 def per_device(nx, ny, hot_ids, hot_grads, cold_grads, cold_slots, cold_counts):

time: 40.7 us -> 40.7 us (level)
  no operation moved by 1% of the time
where the time goes in v4:
time: 40.7 us; the launch traced here: 40.6 us
  Pallas kernels  40 us (98%)
  between operations  0.64 us (2%)
    pallas_call x1, Pallas kernels, per_device(): pl.pallas_call(functools.partial(kernel, nx, ny, factor, *make_waves(ny))...  38.6 us
    pallas_call x1, Pallas kernels, per_device(): pl.pallas_call(store, out_shape=(jax.ShapeDtypeStruct((HOT, width), f32),...  1.33 us

profile of v4, /device:TPU:0, one launch (start us, length us, event | category | flops | bytes accessed | tf_op | source)
XLA Modules:
  0.0 40.6 jit_solution(8658579499609632648)
XLA Ops:
  0.6 38.6 %shard_map.68 = (f32[2048,128]{1,0:T(8,128)S(1)}, f32[2048,128]{1,0:T(8,128)S(1)}) custom-call(s32[8,8,128]{2,1,0:T(8,128)} %bitcast.6, bf16[8192,128]{1,0:T(8,128)(2,1)} %hot_ref.1, s32[8,512]{1,0:T(8,128)} %bitcast.7, s32[8]{0:T(128)} %bitcast.8, bf16[8,512,128]{2,1,0:T(8,128)(2,1)} %bitcast.5), custom_call_target="tpu_custom_call" | custom-call | tf_op jit(solution)/shard_map/pallas_call | solution.py:454
  39.3 1.3 %shard_map.69 = (f32[2048,128]{1,0:T(8,128)}, f32[2048,128]{1,0:T(8,128)}) custom-call(f32[2048,128]{1,0:T(8,128)S(1)} %get-tuple-element.6.hot_ref, f32[2048,128]{1,0:T(8,128)S(1)} %get-tuple-element.7.cold_ref), custom_call_target="tpu_custom_call" | custom-call | tf_op jit(solution)/shard_map/pallas_call | solution.py:497
